TPU v7x, 256 devices: a whole 4x4x8 slice. The times are simulated.
256 devices in a mesh: row: 8 (over z), col: 16 (over y_lo, x, core), layer: 2 (over y_hi).
Axes of the slice: x: 4, y: 4 (y_hi: 2, y_lo: 2; y = y_hi * 2 + y_lo), z: 8, core: 2. Of those that a mesh axis runs over, the one named last changes fastest.
Arguments:
- left: bfloat16 [8192, 8192], P('row', ('col', 'layer')), may hold values from -6 to 6
- middle: bfloat16 [8192, 8192], P('row', 'col'), may hold values from -0.0625 to 0.0625
- right: bfloat16 [8192, 8192], P('row', 'col'), may hold values from -0.0625 to 0.0625
Outputs:
- product: bfloat16 [8192, 8192], P('row', ('col', 'layer'))
All inputs are finite; a program needn't handle non-finite values.
Results may differ from a plain program's by a relative error of at most 0.0049.
Values may be sent and summed in bfloat16 or wider, within the bound.
A program may use at most 64 MiB of HBM per device.

v0:
```python
import jax
import jax.numpy as jnp
from jax import lax
from jax.sharding import PartitionSpec as P


def split_up(array, dim, size):
    lengths = array.shape
    blocks = array.reshape(*lengths[:dim], size, lengths[dim] // size, *lengths[dim + 1 :])
    return jnp.moveaxis(blocks, dim, 0)


def sum_at_owner(array, axis, dim):
    blocks = split_up(array, dim, lax.axis_size(axis))
    arrived = lax.all_to_all(blocks, axis, split_axis=0, concat_axis=0, tiled=True)
    return arrived.sum(axis=0)


def multiply(left, right):
    width = left.shape[1]
    layers = lax.axis_size("layer")
    layer_index = lax.axis_index("layer")
    columns = right.shape[1]
    groups = right.shape[0] // width // layers
    shaped = right.reshape(groups, layers, width, columns)
    own_rows = lax.dynamic_index_in_dim(shaped, layer_index, 1, keepdims=False).reshape(
        groups * width, columns
    )
    right_all = lax.all_gather(own_rows, "row", axis=0, tiled=True)
    return jnp.dot(
        lax.all_gather(left, "col", axis=1, tiled=True),
        right_all,
        preferred_element_type=jnp.float32,
    )


def per_device(left, middle, right):
    partial_value = multiply(left, middle)
    first = sum_at_owner(partial_value, "layer", 1)
    first = first.astype(jnp.bfloat16)
    second = multiply(first, right)
    return sum_at_owner(second, "layer", 1).astype(jnp.bfloat16)


def solution(mesh):
    return jax.shard_map(
        per_device,
        mesh=mesh,
        in_specs=(P("row", ("col", "layer")), P("row", "col"), P("row", "col")),
        out_specs=P("row", ("col", "layer")),
        check_vma=False,
    )
```

profile of v0, /device:TPU:1, one launch (start us, length us, event | category | flops | bytes accessed | tf_op | source)
XLA Modules:
  0.0 290.7 jit_solution(16866077000397679622)
XLA Ops:
  6.5 0.0 copy-start
  6.5 0.0 all-gather.5.cloned.1.call-start
  6.5 1.2 copy-done
  7.8 0.8 constant_dynamic-slice_fusion.1
  8.6 0.0 all-gather.5.cloned.1.call-update
  8.6 0.0 all-gather.7.cloned.1.call-start
  8.7 0.7 all-gather.7.cloned.1.call-update
  9.4 0.0 all-gather.11.cloned.1.call-start
  9.4 1.9 constant_dynamic-slice_fusion
  11.3 0.0 all-gather.11.cloned.1.call-update
  11.3 0.0 all-gather.9.cloned.1.call-start
  11.4 56.2 %all-gather.5.cloned.1.call-done = bf16[4096,512]{1,0:T(8,128)(2,1)} async-done(((bf16[512,512]{1,0:T(8,128)(2,1)}), bf16[4096,512]{1,0:T(8,128)(2,1)}) %all-gather.5.cloned.1.call-update) | async-done | bytes 4194320 | tf_op jit(solution)/shard_map/all_gather | solution.py:29
  67.5 64.4 %all-gather.7.cloned.1.call-done = bf16[1024,4096]{1,0:T(8,128)(2,1)} async-done(((bf16[1024,256]{1,0:T(8,128)(2,1)}), bf16[1024,4096]{1,0:T(8,128)(2,1)}) %all-gather.7.cloned.1.call-update) | async-done | bytes 8388624 | tf_op jit(solution)/shard_map/all_gather | solution.py:31
  131.9 8.2 %fusion = f32[512,1024]{1,0:T(8,128)S(1)} fusion(bf16[4096,512]{1,0:T(8,128)(2,1)} %all-gather.5.cloned.1.call-done, bf16[1024,4096]{1,0:T(8,128)(2,1)} %all-gather.7.cloned.1.call-done), kind=kOutput, calls=%fused_computation.2 | convolution fusion | flops 4294967296 | bytes 14680064 | tf_op jit(solution)/shard_map/dot_general | solution.py:30
  140.1 28.8 %all_to_all.10 = f32[2,1024,256]{1,2,0:T(8,128)S(1)} all-to-all(f32[2,1024,256]{1,2,0:T(8,128)S(1)} %bitcast.17), channel_id=1, replica_groups=mesh['row'=8,'col'=16,'layer'=2] {'layer'}, dimensions={0} | all-to-all | bytes 4194304 | tf_op jit(solution)/shard_map/all_to_all | solution.py:15
  168.9 1.1 reduce_sum.18
  170.0 0.0 all-gather.9.cloned.1.call-update
  170.0 17.7 %all-gather.11.cloned.1.call-done = bf16[4096,512]{1,0:T(8,128)(2,1)} async-done(((bf16[512,512]{1,0:T(8,128)(2,1)}), bf16[4096,512]{1,0:T(8,128)(2,1)}) %all-gather.11.cloned.1.call-update) | async-done | bytes 4194320 | tf_op jit(solution)/shard_map/all_gather | solution.py:29
  187.7 55.5 %all-gather.9.cloned.1.call-done = bf16[1024,4096]{0,1:T(8,128)(2,1)} async-done(((bf16[1024,256]{0,1:T(8,128)(2,1)}), bf16[1024,4096]{0,1:T(8,128)(2,1)}) %all-gather.9.cloned.1.call-update) | async-done | bytes 8388624 | tf_op jit(solution)/shard_map/all_gather | solution.py:31
  243.2 8.2 %fusion.1 = f32[1024,512]{0,1:T(8,128)S(1)} fusion(bf16[1024,4096]{0,1:T(8,128)(2,1)} %all-gather.9.cloned.1.call-done, bf16[4096,512]{1,0:T(8,128)(2,1)} %all-gather.11.cloned.1.call-done), kind=kOutput, calls=%fused_computation.3 | convolution fusion | flops 4294967296 | bytes 14680064 | tf_op jit(solution)/shard_map/dot_general | solution.py:30
  251.4 29.6 %all_to_all.11 = f32[2,1024,256]{1,2,0:T(8,128)S(1)} all-to-all(f32[2,1024,256]{1,2,0:T(8,128)S(1)} %bitcast.18), channel_id=1, replica_groups=mesh['row'=8,'col'=16,'layer'=2] {'layer'}, dimensions={0} | all-to-all | bytes 4194304 | tf_op jit(solution)/shard_map/all_to_all | solution.py:15
  281.0 1.1 reduce_sum.19
  282.1 2.0 copy.4
Async XLA Ops:
  6.5 1.2 copy-start
  6.5 61.0 %all-gather.5.cloned.1.call-start = ((), (), s32[]{:S(2)}) async-start(), calls=%async_computation.2 | async-start | bytes 4718592 | tf_op jit(solution)/shard_map/all_gather | solution.py:29
  8.6 123.3 %all-gather.7.cloned.1.call-start = ((), (), s32[]{:S(2)}) async-start(), calls=%async_computation.3 | async-start | bytes 8912896 | tf_op jit(solution)/shard_map/all_gather | solution.py:31
  9.4 178.3 %all-gather.11.cloned.1.call-start = ((), (), s32[]{:S(2)}) async-start(), calls=%async_computation.5 | async-start | bytes 4718592 | tf_op jit(solution)/shard_map/all_gather | solution.py:29
  11.3 231.9 %all-gather.9.cloned.1.call-start = ((), (), s32[]{:S(2)}) async-start(), calls=%async_computation.4 | async-start | bytes 8912896 | tf_op jit(solution)/shard_map/all_gather | solution.py:31
Sparse Core Ops, SparseCore 0:
  9.1 58.3 all-gather.4
  69.3 62.5 all-gather.6
  133.7 53.9 all-gather.10
  189.4 53.7 all-gather.8
where the time goes:
time: 291 us
  waiting for transfers between devices  194 us (67%)
  blocking collectives  58.3 us (20%)
  matrix products  16.5 us (6%)
  between operations  13.1 us (5%)
  local copies, waits for them, and re-layouts  5.97 us (2%)
    all_gather x2, waiting for transfers between devices, multiply(): lax.all_gather(left, 'col', axis=1, tiled=True)  120 us
    all_gather x2, waiting for transfers between devices, multiply(): right_all = lax.all_gather(own_rows, 'row', axis=0, tiled=True)  73.8 us
    all_to_all x2, blocking collectives, sum_at_owner(): lax.all_to_all(blocks, axis, split_axis=0, concat_axis=0, tiled=True)  58.3 us
    dot_general x2, matrix products, multiply(): jnp.dot(lax.all_gather(left, 'col', axis=1, tiled=True), right_all, prefe...  16.5 us
  transfers between devices with their start and end apart: 4, of which 4 were waited for; matrix products, arithmetic and copies ran while one was open for 4% of the time, Pallas kernels for 0%

commit v1 on v0

v1 whole, which is shorter than its diff:
```python
import jax
import jax.numpy as jnp
from jax import lax
from jax.experimental import pallas as pl
from jax.experimental.pallas import tpu as pltpu
from jax.sharding import PartitionSpec as P

MESH = pl.DeviceIdType.MESH
BF16 = jnp.bfloat16
TM = 256
TILES = 1024 // TM

STAGES = [(0, 0), (0, 1), (0, 2), (0, 3), (1, 0), (1, 1), (1, 2), (1, 3)]

ORDER = [
    (1, 0), (0, 0), (1, 1), (0, 1), (1, 2), (0, 2), (1, 3), (0, 3),
    (2, 0), (3, 0), (2, 1), (3, 1), (2, 2), (3, 2), (2, 3), (4, 0), (3, 3),
    (5, 0), (4, 1), (5, 1), (4, 2), (6, 0), (4, 3), (5, 2), (6, 1), (5, 3), (7, 0),
    (6, 2), (7, 1), (6, 3), (7, 2), (7, 3),
]


def rem(a, n):
    return lax.rem(a + 4 * n, jnp.int32(n))


def kernel(left, middle, right, out, A, B, send, recv, obuf,
           bar_unused, zS, zR, xS, xR, dS, dR, cS, cR, hS, hR, wS, wR, lS, oS):
    z = lax.axis_index("row")
    col = lax.axis_index("col")
    h = lax.axis_index("layer")
    c = lax.rem(col, 2)
    x = lax.rem(lax.div(col, 2), 4)
    lo = lax.div(col, 8)
    y = h * 2 + lo

    def dev(zz=None, xx=None, yy=None, cc=None):
        zz = z if zz is None else zz
        xx = x if xx is None else xx
        yy = y if yy is None else yy
        cc = c if cc is None else cc
        return (zz, lax.rem(yy, 2) * 8 + xx * 2 + cc, lax.div(yy, 2))

    z_to = [dev(zz=rem(z + 1, 8)), dev(zz=rem(z - 1, 8))]
    x_to = [dev(xx=rem(x + 1, 4)), dev(xx=rem(x - 1, 4))]
    y_of = [dev(yy=rem(y + d, 4)) for d in (1, 2, 3)]
    pair = dev(yy=h * 2 + 1 - lo)
    yt = h * 2 + 1 - lo
    core = dev(cc=1 - c)

    barrier = pltpu.get_barrier_semaphore()
    for peer in z_to + x_to + y_of + [core]:
        pl.semaphore_signal(barrier, inc=1, device_id=peer, device_id_type=MESH)

    def m128(v):
        return pl.multiple_of(v, 128)

    def zpos(zz):
        return lax.rem(zz, 4) * 2 + lax.div(zz, 4)

    def local(src, dst, sem):
        return pltpu.make_async_copy(src, dst, sem)

    def remote(src, dst, ssem, rsem, to):
        return pltpu.make_async_remote_copy(
            src_ref=src, dst_ref=dst, send_sem=ssem, recv_sem=rsem, device_id=to, device_id_type=MESH
        )

    ymod = lambda v: rem(v, 4)

    def own_rows(p, j, cols_from, width, cols_to, ywho):
        src = (middle, right)[p].at[:, pl.ds(m128(ywho * 128), 128), pl.ds(m128(cols_from), width)]
        dst = B.at[p, j, :, zpos(z), :, pl.ds(cols_to, width)]
        return src, dst

    def own_parts(yw, l_src):
        own = [
            (0, 1, ymod(yw + 1) * 128, 128, 0),
            (0, 1, ymod(yw + 3) * 128, 128, 128),
            (0, 0, ymod(yw + 2) * 128, 128, m128(l_src * 128)),
            (0, 3, yw * 128, 128, m128(l_src * 128)),
            (1, 0, lax.div(ymod(yw + 2), 2) * 256, 256, 0),
            (1, 3, lax.div(yw, 2) * 256, 256, 0),
        ]
        hop = [
            (0, 0, ymod(yw + 2) * 128, 128, m128(l_src * 128)),
            (0, 2, ymod(yw + 1) * 128, 128, 0),
            (0, 2, ymod(yw + 3) * 128, 128, 128),
            (0, 3, yw * 128, 128, m128(l_src * 128)),
            (1, 1, lax.div(ymod(yw + 1), 2) * 256, 128, 0),
            (1, 1, lax.div(ymod(yw + 3), 2) * 256, 128, 128),
            (1, 2, lax.div(ymod(yw + 1), 2) * 256 + 128, 128, 0),
            (1, 2, lax.div(ymod(yw + 3), 2) * 256 + 128, 128, 128),
        ]
        return own, hop

    own, _ = own_parts(y, lo)
    _, hop_out = own_parts(yt, lo)
    _, hop_in = own_parts(y, 1 - lo)
    own_copies = [local(*own_rows(p, j, f, w, t, y), lS.at[i]) for i, (p, j, f, w, t) in enumerate(own)]
    hop_sends = [
        remote(*own_rows(p, j, f, w, t, yt), hS.at[i], hR.at[i], pair) for i, (p, j, f, w, t) in enumerate(hop_out)
    ]
    hop_recvs = [
        remote(*own_rows(p, j, f, w, t, y), hS.at[i], hR.at[i], pair) for i, (p, j, f, w, t) in enumerate(hop_in)
    ]

    def strip(cc, xx):
        return (cc * 4 + xx) * 256

    def xregion(p, cc, xx, u):
        if p == 0:
            half = lo if u < 2 else 1 - lo
            return A.at[0, pl.ds((u % 2) * 512, 512), pl.ds(m128(strip(cc, xx) + half * 128), 128)]
        return A.at[1, pl.ds(u * TM, TM), pl.ds(m128(strip(cc, xx)), 256)]

    left_copy = local(
        left.at[:, pl.ds(m128(lo * 128), 128)],
        A.at[0, :, pl.ds(m128(strip(c, x) + lo * 128), 128)],
        lS.at[6],
    )
    swaps = [
        remote(
            left.at[pl.ds(u * 512, 512), pl.ds(m128((1 - lo) * 128), 128)],
            A.at[0, pl.ds(u * 512, 512), pl.ds(m128(strip(c, x) + lo * 128), 128)],
            wS.at[u], wR.at[u], pair,
        )
        for u in range(2)
    ]
    swap_recvs = [
        remote(
            left.at[pl.ds(u * 512, 512), pl.ds(m128((1 - lo) * 128), 128)],
            A.at[0, pl.ds(u * 512, 512), pl.ds(m128(strip(c, x) + (1 - lo) * 128), 128)],
            wS.at[u], wR.at[u], pair,
        )
        for u in range(2)
    ]

    left_copy.start()
    for i in range(6):
        own_copies[i].start()

    pl.semaphore_wait(barrier, 8)

    sent = []

    def go(copy):
        copy.start()
        sent.append(copy)

    go(hop_sends[0])
    for u in range(2):
        go(swaps[u])
    for i in range(1, 8):
        go(hop_sends[i])

    OWN_OF = {(0, 0): [2], (0, 1): [0, 1], (0, 2): [], (0, 3): [3], (1, 0): [4], (1, 1): [], (1, 2): [], (1, 3): [5]}
    HOP_OF = {(0, 0): [0], (0, 1): [], (0, 2): [1, 2], (0, 3): [3], (1, 0): [], (1, 1): [4, 5], (1, 2): [6, 7], (1, 3): []}

    def z_copy(s, d, minor, level, arriving):
        p, j = STAGES[s]
        sign = -1 if d == 0 else 1
        half = d if minor == 0 else 1 - d
        block = rem(z + sign * (level + (1 if arriving else 0)), 8)
        ref = B.at[p, j, half, zpos(block)]
        k = level + (4 if minor else 0)
        return remote(ref, ref, zS.at[d, s, k], zR.at[d, s, k], z_to[d])

    def z_tick(s, level):
        if level == 0:
            for i in OWN_OF[STAGES[s]]:
                own_copies[i].wait()
            for i in HOP_OF[STAGES[s]]:
                hop_recvs[i].wait_recv()
        for minor in range(2):
            if minor == 1 and level == 3:
                continue
            for d in range(2):
                if level > 0:
                    z_copy(s, d, minor, level - 1, True).wait_recv()
                go(z_copy(s, d, minor, level, False))

    def z_last(s):
        for d in range(2):
            z_copy(s, d, 1, 2, True).wait_recv()
            z_copy(s, d, 0, 3, True).wait_recv()

    def x_copy(p, d, u, forward, arriving):
        sign = -1 if d == 0 else 1
        away = (1 if forward else 0) + (1 if arriving else 0)
        ref = xregion(p, c, rem(x + sign * away, 4), u)
        k = 4 + u // 2 if forward else u
        return remote(ref, ref, xS.at[p, d, k], xR.at[p, d, k], x_to[d])

    def x_forward(p, d, u):
        x_copy(p, d, u, False, True).wait_recv()
        go(x_copy(p, d, u, True, False))

    def d_copy(p, away, u, arriving):
        cc = 1 - c if arriving else c
        ref = xregion(p, cc, rem(x + away, 4), u)
        return remote(ref, ref, dS.at[p, away, u], dR.at[p, away, u], core)

    def d_all(p):
        for away in range(4):
            for u in range(4):
                d_copy(p, away, u, True).wait_recv()

    def c_copies(p, j, t, arriving):
        rows = pl.ds(t * TM, TM)
        if j == 0:
            return [remote(send.at[p, 0, rows], recv.at[p, 1, rows], cS.at[p, 0, t], cR.at[p, 0, t], y_of[1])]
        made = []
        for q in range(2):
            if p == 0:
                which = lo if (j == 1) != arriving else 1 - lo
                place = m128(which * 128)
            else:
                place = (j - 1) * 128
            k = 1 + (j - 1) * 2 + q
            made.append(
                remote(
                    send.at[p, j, rows, pl.ds(q * 128, 128)],
                    recv.at[p, 2 * q, rows, pl.ds(place, 128)],
                    cS.at[p, k, t], cR.at[p, k, t], y_of[2 * q],
                )
            )
        return made

    def compute(s, t0, t1):
        p, j = STAGES[s]

        def body(t, carry):
            rows = pl.ds(pl.multiple_of(t * TM, TM), TM)
            acc = jnp.dot(A[p, rows, :], B[p, j].reshape(2048, 256), preferred_element_type=jnp.float32)
            if j < 3:
                send[p, j, rows, :] = acc.astype(BF16)
                for copy in c_copies(p, j, t, False):
                    copy.start()
                return carry
            for jj in range(3):
                for copy in c_copies(p, jj, t, True):
                    copy.wait_recv()
            for d in range(3):
                acc = acc + recv[p, d, rows, :].astype(jnp.float32)
            if p == 0:
                A[1, rows, pl.ds(m128(strip(c, x)), 256)] = acc.astype(BF16)
                own_strip = A.at[1, rows, pl.ds(m128(strip(c, x)), 256)]
                for d in range(2):
                    remote(own_strip, own_strip, xS.at[1, d, t], xR.at[1, d, t], x_to[d]).start()
                remote(own_strip, own_strip, dS.at[1, 0, t], dR.at[1, 0, t], core).start()
            else:
                obuf[rows, :] = acc.astype(BF16)
                local(obuf.at[rows], out.at[rows], oS.at[t]).start()
            return carry

        lax.fori_loop(t0, t1, body, 0)

    def x_start_own():
        left_copy.wait()
        for u in (0, 1):
            go(x_copy(0, 0, u, False, False))
            go(x_copy(0, 1, 1 - u, False, False))
            go(d_copy(0, 0, u, False))

    def x_start_swapped():
        for u in (2, 3):
            swap_recvs[u - 2].wait_recv()
        for u in (2, 3):
            go(x_copy(0, 0, u, False, False))
            go(x_copy(0, 1, 5 - u, False, False))
            go(d_copy(0, 0, u, False))

    def x_forwards(p, us):
        for u in us:
            d = u % 2
            x_forward(p, d, u)
            go(d_copy(p, 3 if d == 0 else 1, u, False))

    def x_rest(p, us):
        for u in us:
            d = 1 - u % 2
            x_copy(p, d, u, False, True).wait_recv()
            go(d_copy(p, 3 if d == 0 else 1, u, False))

    def x_far(p, us):
        for u in us:
            x_copy(p, u % 2, u, True, True).wait_recv()
            go(d_copy(p, 2, u, False))

    ACTIONS = {
        0: [x_start_own],
        3: [lambda: x_forwards(0, (0, 1))],
        4: [x_start_swapped, lambda: x_rest(0, (0, 1))],
        6: [lambda: x_forwards(0, (2, 3)), lambda: x_far(0, (0, 1))],
        7: [lambda: x_rest(0, (2, 3))],
        8: [lambda: z_last(1), lambda: z_last(0), lambda: x_far(0, (2, 3))],
        9: [lambda: d_all(0), lambda: compute(0, 0, 2)],
        10: [lambda: compute(0, 2, 4)],
        11: [lambda: compute(1, 0, 2)],
        12: [lambda: compute(1, 2, 4)],
        15: [lambda: z_last(2), lambda: compute(2, 0, 4)],
        17: [lambda: z_last(3), lambda: compute(3, 0, 4)],
        19: [lambda: x_forwards(1, (0, 1))],
        21: [lambda: x_forwards(1, (2, 3)), lambda: x_rest(1, (0, 1))],
        22: [lambda: x_rest(1, (2, 3))],
        23: [lambda: x_far(1, (0, 1))],
        24: [lambda: x_far(1, (2, 3)), lambda: z_last(4), lambda: d_all(1), lambda: compute(4, 0, 2)],
        25: [lambda: compute(4, 2, 4)],
        26: [lambda: z_last(5), lambda: compute(5, 0, 2)],
        27: [lambda: compute(5, 2, 4)],
        30: [lambda: z_last(6), lambda: compute(6, 0, 4)],
        31: [lambda: z_last(7), lambda: compute(7, 0, 4)],
    }
    for i, (s, level) in enumerate(ORDER):
        z_tick(s, level)
        for action in ACTIONS.get(i, ()):
            action()

    for copy in sent:
        copy.wait_send()
    for p in range(2):
        for j in range(3):
            for t in range(TILES):
                for copy in c_copies(p, j, t, False):
                    copy.wait_send()
    for t in range(TILES):
        for d in range(2):
            x_copy(1, d, t, False, False).wait_send()
        d_copy(1, 0, t, False).wait_send()
        local(obuf.at[pl.ds(t * TM, TM)], out.at[pl.ds(t * TM, TM)], oS.at[t]).wait()


def per_device(left, middle, right):
    rows, width = left.shape
    dma = pltpu.SemaphoreType.DMA
    return pl.pallas_call(
        kernel,
        out_shape=jax.ShapeDtypeStruct((rows, width), BF16),
        in_specs=[pl.BlockSpec(memory_space=pl.ANY)] * 3,
        out_specs=pl.BlockSpec(memory_space=pl.ANY),
        scratch_shapes=[
            pltpu.VMEM((2, 1024, 2048), BF16),
            pltpu.VMEM((2, 4, 2, 8, 128, 256), BF16),
            pltpu.VMEM((2, 3, 1024, 256), BF16),
            pltpu.VMEM((2, 3, 1024, 256), BF16),
            pltpu.VMEM((1024, 256), BF16),
            pltpu.SemaphoreType.REGULAR,
            dma((2, 8, 7)), dma((2, 8, 7)),
            dma((2, 2, 6)), dma((2, 2, 6)),
            dma((2, 4, 4)), dma((2, 4, 4)),
            dma((2, 5, TILES)), dma((2, 5, TILES)),
            dma((8,)), dma((8,)),
            dma((2,)), dma((2,)),
            dma((7,)),
            dma((TILES,)),
        ],
        compiler_params=pltpu.CompilerParams(
            collective_id=0, has_side_effects=True, vmem_limit_bytes=60 * 1024 * 1024
        ),
    )(left, middle.reshape(2, rows // 2, -1), right.reshape(2, rows // 2, -1))


def solution(mesh):
    return jax.shard_map(
        per_device,
        mesh=mesh,
        in_specs=(P("row", ("col", "layer")), P("row", "col"), P("row", "col")),
        out_specs=P("row", ("col", "layer")),
        check_vma=False,
    )
```

time: 291 us -> 111 us (0.38)
  waiting for transfers between devices: 194 us -> 0 us
  Pallas kernels: 0 us -> 109 us
  blocking collectives: 58.3 us -> 0 us
  matrix products: 16.5 us -> 0 us
  between operations: 13.1 us -> 0.01 us
  local copies, waits for them, and re-layouts: 5.97 us -> 1.87 us
    all_gather x4 -> x0, waiting for transfers between devices: 194 us -> none  [the longest x2 120 us: multiply(): lax.all_gather(left, 'col', axis=1, tiled=True)]
    pallas_call x0 -> x1, Pallas kernels: none -> 109 us  [per_device(): pl.pallas_call(kernel, out_shape=jax.ShapeDtypeStruct((rows, width), BF16...]
    all_to_all x2 -> x0, blocking collectives: 58.3 us -> none  [sum_at_owner(): lax.all_to_all(blocks, axis, split_axis=0, concat_axis=0, tiled=True)]
    dot_general x2 -> x0, matrix products: 16.5 us -> none  [multiply(): jnp.dot(lax.all_gather(left, 'col', axis=1, tiled=True), right_all, prefe...]
  transfers between devices with their start and end apart: 4 -> 0, of which waited for: 4 -> 0; matrix products, arithmetic and copies ran while one was open for 4% -> 0% of each run, Pallas kernels for 0% -> 0%
where the time goes in v1:
time: 111 us; the launch traced here: 110 us
  Pallas kernels  109 us (98%)
  local copies, waits for them, and re-layouts  1.87 us (2%)
    pallas_call x1, Pallas kernels, per_device(): pl.pallas_call(kernel, out_shape=jax.ShapeDtypeStruct((rows, width), BF16...  109 us

profile of v1, /device:TPU:1, one launch (start us, length us, event | category | flops | bytes accessed | tf_op | source)
XLA Modules:
  0.0 110.4 jit_solution(3711164786377078737)
XLA Ops:
  0.0 108.5 %shard_map.37 = bf16[1024,256]{1,0:T(8,128)(2,1)} custom-call(bf16[1024,256]{1,0:T(8,128)(2,1)} %left.1, bf16[2,512,512]{2,1,0:T(8,128)(2,1)} %bitcast.2, bf16[2,512,512]{2,1,0:T(8,128)(2,1)} %bitcast.3), custom_call_target="tpu_custom_call" | custom-call | tf_op jit(solution)/shard_map/pallas_call | solution.py:337
  108.5 1.9 %copy.5 = bf16[1024,256]{1,0:T(8,128)(2,1)} copy(bf16[1024,256]{1,0:T(8,128)(2,1)} %shard_map.37) | data formatting | bytes 1048576

commit v2 on v1

v2 whole, which is shorter than its diff:
```python
import jax
import jax.numpy as jnp
from jax import lax
from jax.experimental import pallas as pl
from jax.experimental.pallas import tpu as pltpu
from jax.sharding import PartitionSpec as P

MESH = pl.DeviceIdType.MESH
BF16 = jnp.bfloat16
TM = 256
TILES = 1024 // TM
UNITS = (4, 8)

STAGES = [(0, 0), (0, 1), (0, 2), (0, 3), (1, 0), (1, 1), (1, 2), (1, 3)]

ORDER = [
    (1, 0), (0, 0), (1, 1), (0, 1), (1, 2), (0, 2), (1, 3), (2, 0), (0, 3), (2, 1), (3, 0),
    (2, 2), (3, 1), (2, 3), (3, 2), (4, 0), (3, 3), (4, 1), (5, 0), (4, 2), (5, 1), (4, 3),
    (6, 0), (5, 2), (6, 1), (5, 3), (7, 0), (6, 2), (7, 1), (6, 3), (7, 2), (7, 3),
]
LAST = 7


def rem(a, n):
    return lax.rem(a + 4 * n, jnp.int32(n))


def kernel(left, middle, right, out, A, B, Bx, own_sum, send, recv,
           zS, zR, xS, xR, dS, dR, cS, cR, hS, hR, wS, wR, lS):
    z = lax.axis_index("row")
    col = lax.axis_index("col")
    h = lax.axis_index("layer")
    c = lax.rem(col, 2)
    x = lax.rem(lax.div(col, 2), 4)
    lo = lax.div(col, 8)
    y = h * 2 + lo

    def dev(zz=None, xx=None, yy=None, cc=None):
        zz = z if zz is None else zz
        xx = x if xx is None else xx
        yy = y if yy is None else yy
        cc = c if cc is None else cc
        return (zz, lax.rem(yy, 2) * 8 + xx * 2 + cc, lax.div(yy, 2))

    z_to = [dev(zz=rem(z + 1, 8)), dev(zz=rem(z - 1, 8))]
    x_to = [dev(xx=rem(x + 1, 4)), dev(xx=rem(x - 1, 4))]
    y_of = [dev(yy=rem(y + d, 4)) for d in (1, 2, 3)]
    pair = dev(yy=h * 2 + 1 - lo)
    yt = h * 2 + 1 - lo
    core = dev(cc=1 - c)

    barrier = pltpu.get_barrier_semaphore()
    for peer in z_to + x_to + y_of + [core]:
        pl.semaphore_signal(barrier, inc=1, device_id=peer, device_id_type=MESH)

    def m128(v):
        return pl.multiple_of(v, 128)

    def zpos(zz):
        return lax.rem(zz, 4) * 2 + lax.div(zz, 4)

    def local(src, dst, sem):
        return pltpu.make_async_copy(src, dst, sem)

    def remote(src, dst, ssem, rsem, to):
        return pltpu.make_async_remote_copy(
            src_ref=src, dst_ref=dst, send_sem=ssem, recv_sem=rsem, device_id=to, device_id_type=MESH
        )

    ymod = lambda v: rem(v, 4)

    def own_rows(p, j, cols_from, width, cols_to, ywho):
        src = (middle, right)[p].at[:, pl.ds(m128(ywho * 128), 128), pl.ds(m128(cols_from), width)]
        dst = B.at[p, j, :, zpos(z), :, pl.ds(cols_to, width)]
        return src, dst

    def own_parts(yw, l_src):
        own = [
            (0, 1, ymod(yw + 1) * 128, 128, 0),
            (0, 1, ymod(yw + 3) * 128, 128, 128),
            (0, 0, ymod(yw + 2) * 128, 128, m128(l_src * 128)),
            (0, 3, yw * 128, 128, m128(l_src * 128)),
            (1, 0, lax.div(ymod(yw + 2), 2) * 256, 256, 0),
            (1, 3, lax.div(yw, 2) * 256, 256, 0),
        ]
        hop = [
            (0, 0, ymod(yw + 2) * 128, 128, m128(l_src * 128)),
            (0, 2, ymod(yw + 1) * 128, 128, 0),
            (0, 2, ymod(yw + 3) * 128, 128, 128),
            (0, 3, yw * 128, 128, m128(l_src * 128)),
            (1, 1, lax.div(ymod(yw + 1), 2) * 256, 128, 0),
            (1, 1, lax.div(ymod(yw + 3), 2) * 256, 128, 128),
            (1, 2, lax.div(ymod(yw + 1), 2) * 256 + 128, 128, 0),
            (1, 2, lax.div(ymod(yw + 3), 2) * 256 + 128, 128, 128),
        ]
        return own, hop

    own, _ = own_parts(y, lo)
    _, hop_out = own_parts(yt, lo)
    _, hop_in = own_parts(y, 1 - lo)
    own_copies = [local(*own_rows(p, j, f, w, t, y), lS.at[i]) for i, (p, j, f, w, t) in enumerate(own)]
    hop_sends = [
        remote(*own_rows(p, j, f, w, t, yt), hS, hR.at[i], pair) for i, (p, j, f, w, t) in enumerate(hop_out)
    ]
    hop_recvs = [
        remote(*own_rows(p, j, f, w, t, y), hS, hR.at[i], pair) for i, (p, j, f, w, t) in enumerate(hop_in)
    ]

    def strip(cc, xx):
        return (cc * 4 + xx) * 256

    def xregion(p, cc, xx, u):
        if p == 0:
            half = lo if u < 2 else 1 - lo
            return A.at[0, pl.ds((u % 2) * 512, 512), pl.ds(m128(strip(cc, xx) + half * 128), 128)]
        return A.at[1, pl.ds(pl.multiple_of(u * 128, 128), 128), pl.ds(m128(strip(cc, xx)), 256)]

    left_copy = local(
        left.at[:, pl.ds(m128(lo * 128), 128)],
        A.at[0, :, pl.ds(m128(strip(c, x) + lo * 128), 128)],
        lS.at[6],
    )
    swaps = [
        remote(
            left.at[pl.ds(u * 512, 512), pl.ds(m128((1 - lo) * 128), 128)],
            A.at[0, pl.ds(u * 512, 512), pl.ds(m128(strip(c, x) + lo * 128), 128)],
            wS, wR.at[u], pair,
        )
        for u in range(2)
    ]
    swap_recvs = [
        remote(
            left.at[pl.ds(u * 512, 512), pl.ds(m128((1 - lo) * 128), 128)],
            A.at[0, pl.ds(u * 512, 512), pl.ds(m128(strip(c, x) + (1 - lo) * 128), 128)],
            wS, wR.at[u], pair,
        )
        for u in range(2)
    ]

    left_copy.start()
    for i in range(6):
        own_copies[i].start()

    for half in range(2):
        B[1, 3, half, zpos(rem(z + 4, 8))] = jnp.zeros((128, 256), BF16)

    pl.semaphore_wait(barrier, 8)

    hop_sends[0].start()
    for u in range(2):
        swaps[u].start()
    for i in range(1, 8):
        hop_sends[i].start()

    OWN_OF = {(0, 0): [2], (0, 1): [0, 1], (0, 2): [], (0, 3): [3], (1, 0): [4], (1, 1): [], (1, 2): [], (1, 3): [5]}
    HOP_OF = {(0, 0): [0], (0, 1): [], (0, 2): [1, 2], (0, 3): [3], (1, 0): [], (1, 1): [4, 5], (1, 2): [6, 7], (1, 3): []}

    def z_copy(s, d, minor, level, arriving):
        p, j = STAGES[s]
        sign = -1 if d == 0 else 1
        half = d if minor == 0 else 1 - d
        block = rem(z + sign * (level + (1 if arriving else 0)), 8)
        ref = B.at[p, j, half, zpos(block)]
        k = level + (4 if minor else 0)
        if s == LAST and level == 3:
            return remote(ref, Bx.at[half], zS.at[p], zR.at[d, s, k], z_to[d])
        return remote(ref, ref, zS.at[p], zR.at[d, s, k], z_to[d])

    def z_tick(s, level):
        if level == 0:
            for i in OWN_OF[STAGES[s]]:
                own_copies[i].wait()
            for i in HOP_OF[STAGES[s]]:
                hop_recvs[i].wait_recv()
        for minor in range(2):
            if minor == 1 and level == 3:
                continue
            for d in range(2):
                if level > 0:
                    z_copy(s, d, minor, level - 1, True).wait_recv()
                z_copy(s, d, minor, level, False).start()

    def z_minor(s):
        for d in range(2):
            z_copy(s, d, 1, 2, True).wait_recv()

    def z_major(s):
        for d in range(2):
            z_copy(s, d, 0, 3, True).wait_recv()

    def z_last(s):
        z_minor(s)
        z_major(s)

    def x_copy(p, d, u, forward, arriving):
        sign = -1 if d == 0 else 1
        away = (1 if forward else 0) + (1 if arriving else 0)
        ref = xregion(p, c, rem(x + sign * away, 4), u)
        k = UNITS[p] + u // 2 if forward else u
        return remote(ref, ref, xS.at[p], xR.at[p * 12 + d * (6, 12)[p] + k], x_to[d])

    def x_forward(p, d, u):
        x_copy(p, d, u, False, True).wait_recv()
        x_copy(p, d, u, True, False).start()

    def d_copy(p, away, g, arriving):
        cc, xx = 1 - c if arriving else c, rem(x + away, 4)
        if p == 0:
            half = lo if g == 0 else 1 - lo
            ref = A.at[0, :, pl.ds(m128(strip(cc, xx) + half * 128), 128)]
        else:
            ref = A.at[1, pl.ds(pl.multiple_of(g * TM, TM), TM), pl.ds(m128(strip(cc, xx)), 256)]
        return remote(ref, ref, dS.at[p], dR.at[p * 8 + away * (2, 4)[p] + g], core)

    def d_all(p, gs):
        for away in range(4):
            for g in gs:
                d_copy(p, away, g, True).wait_recv()

    def x_send_tile(t):
        for u in range(2 * t, 2 * t + 2):
            x_copy(1, 0, u, False, False).start()
            x_copy(1, 1, 4 * t + 1 - u, False, False).start()

    def c_copies(p, j, t, arriving):
        rows = pl.ds(t * TM, TM)
        if j == 0:
            return [remote(send.at[p, 0, rows], recv.at[p, 1, rows], cS.at[p], cR.at[p, 0, t], y_of[1])]
        made = []
        for q in range(2):
            if p == 0:
                which = lo if (j == 1) != arriving else 1 - lo
                place = m128(which * 128)
            else:
                place = (j - 1) * 128
            k = 1 + (j - 1) * 2 + q
            made.append(
                remote(
                    send.at[p, j, rows, pl.ds(q * 128, 128)],
                    recv.at[p, 2 * q, rows, pl.ds(place, 128)],
                    cS.at[p], cR.at[p, k, t], y_of[2 * q],
                )
            )
        return made

    def compute(s, t0, t1):
        p, j = STAGES[s]

        def body(t, carry):
            rows = pl.ds(pl.multiple_of(t * TM, TM), TM)
            acc = jnp.dot(A[p, rows, :], B[p, j].reshape(2048, 256), preferred_element_type=jnp.float32)
            if j < 3:
                send[p, j, rows, :] = acc.astype(BF16)
                for copy in c_copies(p, j, t, False):
                    copy.start()
                return carry
            if s == LAST:
                own_sum[rows, :] = acc
                return carry
            finish(p, t, rows, acc)
            return carry

        lax.fori_loop(t0, t1, body, 0)

    def finish_last(t0, t1):
        def body(t, carry):
            rows = pl.ds(pl.multiple_of(t * TM, TM), TM)
            far = zpos(rem(z + 4, 8))
            piece = jnp.concatenate(
                [A[1, rows, pl.ds(m128((half * 8 + far) * 128), 128)] for half in range(2)], axis=1
            )
            acc = jnp.dot(piece, Bx[...].reshape(256, 256), preferred_element_type=jnp.float32)
            finish(1, t, rows, own_sum[rows, :] + acc)
            return carry

        lax.fori_loop(t0, t1, body, 0)

    def finish(p, t, rows, acc):
        if True:
            for jj in range(3):
                for copy in c_copies(p, jj, t, True):
                    copy.wait_recv()
            for d in range(3):
                acc = acc + recv[p, d, rows, :].astype(jnp.float32)
            if p == 0:
                A[1, rows, pl.ds(m128(strip(c, x)), 256)] = acc.astype(BF16)
                d_copy(1, 0, t, False).start()
            else:
                out[rows, :] = acc.astype(BF16)

    def x_start(u):
        if u == 0:
            left_copy.wait()
        if u >= 2:
            swap_recvs[u - 2].wait_recv()
        for d in range(2):
            x_copy(0, d, u, False, False).start()
        if u % 2 == 1:
            d_copy(0, 0, u // 2, False).start()

    def x_forwards(p, us):
        for u in us:
            x_forward(p, u % 2, u)

    def x_rest(p, g):
        for u in (2 * g, 2 * g + 1):
            x_copy(p, 1 - u % 2, u, False, True).wait_recv()
        for away in (1, 3):
            d_copy(p, away, g, False).start()

    def x_far(p, g):
        for u in (2 * g, 2 * g + 1):
            x_copy(p, u % 2, u, True, True).wait_recv()
        d_copy(p, 2, g, False).start()

    def do(f, *args):
        return lambda: f(*args)

    ACTIONS = {
        0: [do(x_start, 0), do(x_start, 1)],
        1: [do(x_forwards, 0, (0, 1))],
        2: [do(x_start, 2), do(x_rest, 0, 0)],
        3: [do(x_start, 3), do(x_far, 0, 0)],
        4: [do(x_forwards, 0, (2,))],
        5: [do(x_forwards, 0, (3,))],
        7: [do(x_rest, 0, 1)],
        8: [do(x_far, 0, 1), do(d_all, 0, (0, 1))],
        10: [do(z_last, 1), do(compute, 1, 0, 4), do(z_last, 0), do(compute, 0, 0, 2)],
        11: [do(compute, 0, 2, 4)],
        15: [do(z_last, 2), do(compute, 2, 0, 4)],
        18: [do(z_last, 3)],
        19: [do(compute, 3, 0, 1), do(x_send_tile, 0), do(compute, 3, 1, 2), do(x_send_tile, 1), do(compute, 3, 2, 4)],
        20: [do(x_forwards, 1, (0, 1)), do(x_send_tile, 2)],
        22: [do(x_forwards, 1, (2, 3)), do(x_send_tile, 3), do(x_rest, 1, 0), do(x_rest, 1, 1)],
        23: [do(x_far, 1, 0), do(x_forwards, 1, (4, 5)), do(z_last, 4), do(d_all, 1, (0,)), do(compute, 4, 0, 1)],
        24: [do(x_rest, 1, 2), do(x_far, 1, 1), do(d_all, 1, (1,)), do(compute, 4, 1, 2)],
        26: [do(x_forwards, 1, (6, 7)), do(x_rest, 1, 3), do(x_far, 1, 2), do(d_all, 1, (2,)),
             do(compute, 4, 2, 3), do(x_far, 1, 3)],
        27: [do(d_all, 1, (3,)), do(compute, 4, 3, 4), do(z_last, 5), do(compute, 5, 0, 4)],
        30: [do(z_last, 6), do(compute, 6, 0, 3)],
        31: [do(compute, 6, 3, 4), do(z_minor, 7), do(compute, 7, 0, 4), do(z_major, 7), do(finish_last, 0, 4)],
    }
    for i, (s, level) in enumerate(ORDER):
        z_tick(s, level)
        for action in ACTIONS.get(i, ()):
            action()

    def all_sent(ref, sem):
        remote(ref, ref, sem, sem, core).wait_send()

    all_sent(B.at[0, 0, 0], hS)
    all_sent(A.at[0, pl.ds(0, 64)], wS)
    for p in range(2):
        all_sent(B.at[p, :, :, pl.ds(0, 7)], zS.at[p])
        all_sent(A.at[p, pl.ds(0, 384)], xS.at[p])
        all_sent(A.at[p, pl.ds(0, 512)], dS.at[p])
        all_sent(send.at[p], cS.at[p])


def per_device(left, middle, right):
    rows, width = left.shape
    dma = pltpu.SemaphoreType.DMA
    return pl.pallas_call(
        kernel,
        out_shape=jax.ShapeDtypeStruct((rows, width), BF16),
        in_specs=[pl.BlockSpec(memory_space=pl.ANY)] * 3,
        out_specs=pl.BlockSpec(memory_space=pltpu.VMEM),
        scratch_shapes=[
            pltpu.VMEM((2, 1024, 2048), BF16),
            pltpu.VMEM((2, 4, 2, 8, 128, 256), BF16),
            pltpu.VMEM((2, 128, 256), BF16),
            pltpu.VMEM((1024, 256), jnp.float32),
            pltpu.VMEM((2, 3, 1024, 256), BF16),
            pltpu.VMEM((2, 3, 1024, 256), BF16),
            dma((2,)), dma((2, 8, 7)),
            dma((2,)), dma((36,)),
            dma((2,)), dma((24,)),
            dma((2,)), dma((2, 5, TILES)),
            dma(()), dma((8,)),
            dma(()), dma((2,)),
            dma((7,)),
        ],
        compiler_params=pltpu.CompilerParams(
            collective_id=0, has_side_effects=True, vmem_limit_bytes=int(62 * 1024 * 1024)
        ),
    )(left, middle.reshape(2, rows // 2, -1), right.reshape(2, rows // 2, -1))


def solution(mesh):
    return jax.shard_map(
        per_device,
        mesh=mesh,
        in_specs=(P("row", ("col", "layer")), P("row", "col"), P("row", "col")),
        out_specs=P("row", ("col", "layer")),
        check_vma=False,
    )
```

time: 111 us -> 102 us (0.919)
  Pallas kernels: 109 us -> 100 us
    pallas_call x1, Pallas kernels: 109 us -> 100 us  [per_device(): pl.pallas_call(kernel, out_shape=jax.ShapeDtypeStruct((rows, width), BF16...]
where the time goes in v2:
time: 102 us
  Pallas kernels  100 us (98%)
  local copies, waits for them, and re-layouts  1.87 us (2%)
    pallas_call x1, Pallas kernels, per_device(): pl.pallas_call(kernel, out_shape=jax.ShapeDtypeStruct((rows, width), BF16...  100 us

profile of v2, /device:TPU:1, one launch (start us, length us, event | category | flops | bytes accessed | tf_op | source)
XLA Modules:
  0.0 102.0 jit_solution(13008131200464155823)
XLA Ops:
  0.0 100.1 %shard_map.37 = bf16[1024,256]{1,0:T(8,128)(2,1)} custom-call(bf16[1024,256]{1,0:T(8,128)(2,1)} %left.1, bf16[2,512,512]{2,1,0:T(8,128)(2,1)} %bitcast.2, bf16[2,512,512]{2,1,0:T(8,128)(2,1)} %bitcast.3), custom_call_target="tpu_custom_call" | custom-call | tf_op jit(solution)/shard_map/pallas_call | solution.py:363
  100.1 1.9 %copy.5 = bf16[1024,256]{1,0:T(8,128)(2,1)} copy(bf16[1024,256]{1,0:T(8,128)(2,1)} %shard_map.37) | data formatting | bytes 1048576

commit v3 on v2

--- a/solution.py
+++ b/solution.py
@@ -15,9 +15,11 @@
 
 ORDER = [
     (1, 0), (0, 0), (1, 1), (0, 1), (1, 2), (0, 2), (1, 3), (2, 0), (0, 3), (2, 1), (3, 0),
-    (2, 2), (3, 1), (2, 3), (3, 2), (4, 0), (3, 3), (4, 1), (5, 0), (4, 2), (5, 1), (4, 3),
-    (6, 0), (5, 2), (6, 1), (5, 3), (7, 0), (6, 2), (7, 1), (6, 3), (7, 2), (7, 3),
+    (2, 2), (3, 1), (2, 3), (3, 2), (3, 3), (4, 0), (4, 1), (5, 0), (4, 2), (5, 1), (4, 3),
+    (6, 0), (5, 2), (6, 1), (5, 3), (6, 2), (7, 0), (6, 3), (7, 1), (7, 2), (7, 3),
 ]
+PARTS = (1, 1, 1, 2, 2, 1, 1, 2)
+FIRST = [sum(14 * n for n in PARTS[:s]) for s in range(9)]
 LAST = 7
 
 
@@ -155,16 +157,16 @@
     OWN_OF = {(0, 0): [2], (0, 1): [0, 1], (0, 2): [], (0, 3): [3], (1, 0): [4], (1, 1): [], (1, 2): [], (1, 3): [5]}
     HOP_OF = {(0, 0): [0], (0, 1): [], (0, 2): [1, 2], (0, 3): [3], (1, 0): [], (1, 1): [4, 5], (1, 2): [6, 7], (1, 3): []}
 
-    def z_copy(s, d, minor, level, arriving):
+    def z_copy(s, d, minor, level, part, arriving):
         p, j = STAGES[s]
         sign = -1 if d == 0 else 1
         half = d if minor == 0 else 1 - d
         block = rem(z + sign * (level + (1 if arriving else 0)), 8)
-        ref = B.at[p, j, half, zpos(block)]
-        k = level + (4 if minor else 0)
-        if s == LAST and level == 3:
-            return remote(ref, Bx.at[half], zS.at[p], zR.at[d, s, k], z_to[d])
-        return remote(ref, ref, zS.at[p], zR.at[d, s, k], z_to[d])
+        rows = pl.ds(part * (128 // PARTS[s]), 128 // PARTS[s])
+        src = B.at[p, j, half, zpos(block), rows]
+        dst = Bx.at[half, rows] if s == LAST and level == 3 else src
+        k = FIRST[s] + (d * 7 + level + (4 if minor else 0)) * PARTS[s] + part
+        return remote(src, dst, zS.at[p], zR.at[k], z_to[d])
 
     def z_tick(s, level):
         if level == 0:
@@ -172,21 +174,22 @@
                 own_copies[i].wait()
             for i in HOP_OF[STAGES[s]]:
                 hop_recvs[i].wait_recv()
-        for minor in range(2):
-            if minor == 1 and level == 3:
-                continue
+        for minor in range(1 if level == 3 else 2):
+            for part in range(PARTS[s]):
+                for d in range(2):
+                    if level > 0:
+                        z_copy(s, d, minor, level - 1, part, True).wait_recv()
+                    z_copy(s, d, minor, level, part, False).start()
+
+    def z_minor(s):
+        for part in range(PARTS[s]):
             for d in range(2):
-                if level > 0:
-                    z_copy(s, d, minor, level - 1, True).wait_recv()
-                z_copy(s, d, minor, level, False).start()
-
-    def z_minor(s):
-        for d in range(2):
-            z_copy(s, d, 1, 2, True).wait_recv()
+                z_copy(s, d, 1, 2, part, True).wait_recv()
 
     def z_major(s):
-        for d in range(2):
-            z_copy(s, d, 0, 3, True).wait_recv()
+        for part in range(PARTS[s]):
+            for d in range(2):
+                z_copy(s, d, 0, 3, part, True).wait_recv()
 
     def z_last(s):
         z_minor(s)
@@ -247,7 +250,7 @@
         p, j = STAGES[s]
 
         def body(t, carry):
-            rows = pl.ds(pl.multiple_of(t * TM, TM), TM)
+            rows = pl.ds(t * TM if isinstance(t, int) else pl.multiple_of(t * TM, TM), TM)
             acc = jnp.dot(A[p, rows, :], B[p, j].reshape(2048, 256), preferred_element_type=jnp.float32)
             if j < 3:
                 send[p, j, rows, :] = acc.astype(BF16)
@@ -260,11 +263,15 @@
             finish(p, t, rows, acc)
             return carry
 
+        if s == LAST:
+            for t in range(t0, t1):
+                body(t, 0)
+            return
         lax.fori_loop(t0, t1, body, 0)
 
     def finish_last(t0, t1):
         def body(t, carry):
-            rows = pl.ds(pl.multiple_of(t * TM, TM), TM)
+            rows = pl.ds(t * TM if isinstance(t, int) else pl.multiple_of(t * TM, TM), TM)
             far = zpos(rem(z + 4, 8))
             piece = jnp.concatenate(
                 [A[1, rows, pl.ds(m128((half * 8 + far) * 128), 128)] for half in range(2)], axis=1
@@ -324,21 +331,25 @@
         4: [do(x_forwards, 0, (2,))],
         5: [do(x_forwards, 0, (3,))],
         7: [do(x_rest, 0, 1)],
-        8: [do(x_far, 0, 1), do(d_all, 0, (0, 1))],
-        10: [do(z_last, 1), do(compute, 1, 0, 4), do(z_last, 0), do(compute, 0, 0, 2)],
+        8: [do(x_far, 0, 1)],
+        10: [do(z_last, 1), do(d_all, 0, (0, 1)), do(compute, 1, 0, 4), do(z_last, 0), do(compute, 0, 0, 2)],
         11: [do(compute, 0, 2, 4)],
-        15: [do(z_last, 2), do(compute, 2, 0, 4)],
-        18: [do(z_last, 3)],
-        19: [do(compute, 3, 0, 1), do(x_send_tile, 0), do(compute, 3, 1, 2), do(x_send_tile, 1), do(compute, 3, 2, 4)],
-        20: [do(x_forwards, 1, (0, 1)), do(x_send_tile, 2)],
-        22: [do(x_forwards, 1, (2, 3)), do(x_send_tile, 3), do(x_rest, 1, 0), do(x_rest, 1, 1)],
-        23: [do(x_far, 1, 0), do(x_forwards, 1, (4, 5)), do(z_last, 4), do(d_all, 1, (0,)), do(compute, 4, 0, 1)],
-        24: [do(x_rest, 1, 2), do(x_far, 1, 1), do(d_all, 1, (1,)), do(compute, 4, 1, 2)],
-        26: [do(x_forwards, 1, (6, 7)), do(x_rest, 1, 3), do(x_far, 1, 2), do(d_all, 1, (2,)),
-             do(compute, 4, 2, 3), do(x_far, 1, 3)],
-        27: [do(d_all, 1, (3,)), do(compute, 4, 3, 4), do(z_last, 5), do(compute, 5, 0, 4)],
-        30: [do(z_last, 6), do(compute, 6, 0, 3)],
-        31: [do(compute, 6, 3, 4), do(z_minor, 7), do(compute, 7, 0, 4), do(z_major, 7), do(finish_last, 0, 4)],
+        14: [do(z_last, 2), do(compute, 2, 0, 1)],
+        16: [do(compute, 2, 1, 4)],
+        18: [do(z_last, 3), do(compute, 3, 0, 1), do(x_send_tile, 0), do(compute, 3, 1, 2), do(x_send_tile, 1),
+             do(compute, 3, 2, 3)],
+        19: [do(compute, 3, 3, 4), do(x_forwards, 1, (0, 1)), do(x_send_tile, 2)],
+        20: [do(x_forwards, 1, (2, 3)), do(x_send_tile, 3), do(x_rest, 1, 0)],
+        22: [do(x_rest, 1, 1), do(x_far, 1, 0)],
+        23: [do(x_forwards, 1, (4, 5)), do(z_last, 4), do(d_all, 1, (0,)), do(compute, 4, 0, 1), do(x_far, 1, 1)],
+        24: [do(x_rest, 1, 2), do(x_forwards, 1, (6, 7)), do(d_all, 1, (1,)), do(compute, 4, 1, 2)],
+        25: [do(x_far, 1, 2)],
+        26: [do(x_rest, 1, 3)],
+        27: [do(d_all, 1, (2,)), do(compute, 4, 2, 3), do(x_far, 1, 3), do(z_last, 5), do(compute, 5, 0, 2), do(d_all, 1, (3,)),
+             do(compute, 4, 3, 4), do(compute, 5, 2, 4)],
+        29: [do(z_last, 6), do(compute, 6, 0, 1)],
+        30: [do(compute, 6, 1, 4)],
+        31: [do(z_minor, 7), do(compute, 7, 0, 4), do(z_major, 7), do(finish_last, 0, 4)],
     }
     for i, (s, level) in enumerate(ORDER):
         z_tick(s, level)
@@ -372,7 +383,7 @@
             pltpu.VMEM((1024, 256), jnp.float32),
             pltpu.VMEM((2, 3, 1024, 256), BF16),
             pltpu.VMEM((2, 3, 1024, 256), BF16),
-            dma((2,)), dma((2, 8, 7)),
+            dma((2,)), dma((FIRST[8],)),
             dma((2,)), dma((36,)),
             dma((2,)), dma((24,)),
             dma((2,)), dma((2, 5, TILES)),
@@ -381,7 +392,7 @@
             dma((7,)),
         ],
         compiler_params=pltpu.CompilerParams(
-            collective_id=0, has_side_effects=True, vmem_limit_bytes=int(62 * 1024 * 1024)
+            collective_id=0, has_side_effects=True, vmem_limit_bytes=int(52 * 1024 * 1024)
         ),
     )(left, middle.reshape(2, rows // 2, -1), right.reshape(2, rows // 2, -1))
 

time: 102 us -> 99.4 us (0.975)
  Pallas kernels: 100 us -> 97.5 us
    pallas_call x1, Pallas kernels: 100 us -> 97.5 us  [per_device(): pl.pallas_call(kernel, out_shape=jax.ShapeDtypeStruct((rows, width), BF16...]
where the time goes in v3:
time: 99.4 us; the launch traced here: 99.3 us
  Pallas kernels  97.5 us (98%)
  local copies, waits for them, and re-layouts  1.84 us (2%)
    pallas_call x1, Pallas kernels, per_device(): pl.pallas_call(kernel, out_shape=jax.ShapeDtypeStruct((rows, width), BF16...  97.5 us

profile of v3, /device:TPU:1, one launch (start us, length us, event | category | flops | bytes accessed | tf_op | source)
XLA Modules:
  0.0 99.3 jit_solution(11472669934407174624)
XLA Ops:
  0.0 0.0 copy-start
  0.0 1.0 %copy-done = bf16[1024,256]{1,0:T(8,128)(2,1)S(1)} copy-done((bf16[1024,256]{1,0:T(8,128)(2,1)S(1)}, bf16[1024,256]{1,0:T(8,128)(2,1)}, u32[]{:S(2)}) %copy-start) | copy-done | bytes 524312
  1.0 97.5 %shard_map.37 = bf16[1024,256]{1,0:T(8,128)(2,1)S(1)} custom-call(bf16[1024,256]{1,0:T(8,128)(2,1)S(1)} %copy-done, bf16[2,512,512]{2,1,0:T(8,128)(2,1)} %bitcast.2, bf16[2,512,512]{2,1,0:T(8,128)(2,1)} %bitcast.3), custom_call_target="tpu_custom_call" | custom-call | tf_op jit(solution)/shard_map/pallas_call | solution.py:374
  98.5 0.8 copy.5
Async XLA Ops:
  0.0 1.0 %copy-start = (bf16[1024,256]{1,0:T(8,128)(2,1)S(1)}, bf16[1024,256]{1,0:T(8,128)(2,1)}, u32[]{:S(2)}) copy-start(bf16[1024,256]{1,0:T(8,128)(2,1)} %left.1) | copy-start | bytes 1572868

commit v4 on v3

--- a/solution.py
+++ b/solution.py
@@ -16,7 +16,7 @@
 ORDER = [
     (1, 0), (0, 0), (1, 1), (0, 1), (1, 2), (0, 2), (1, 3), (2, 0), (0, 3), (2, 1), (3, 0),
     (2, 2), (3, 1), (2, 3), (3, 2), (3, 3), (4, 0), (4, 1), (5, 0), (4, 2), (5, 1), (4, 3),
-    (6, 0), (5, 2), (6, 1), (5, 3), (6, 2), (7, 0), (6, 3), (7, 1), (7, 2), (7, 3),
+    (6, 0), (5, 2), (6, 1), (5, 3), (7, 0), (6, 2), (7, 1), (6, 3), (7, 2), (7, 3),
 ]
 PARTS = (1, 1, 1, 2, 2, 1, 1, 2)
 FIRST = [sum(14 * n for n in PARTS[:s]) for s in range(9)]
@@ -27,7 +27,7 @@
     return lax.rem(a + 4 * n, jnp.int32(n))
 
 
-def kernel(left, middle, right, out, A, B, Bx, own_sum, send, recv,
+def kernel(left, middle, right, out, A, B, Bx, own_sum, send, recv, relay,
            zS, zR, xS, xR, dS, dR, cS, cR, hS, hR, wS, wR, lS):
     z = lax.axis_index("row")
     col = lax.axis_index("col")
@@ -80,13 +80,13 @@
         own = [
             (0, 1, ymod(yw + 1) * 128, 128, 0),
             (0, 1, ymod(yw + 3) * 128, 128, 128),
-            (0, 0, ymod(yw + 2) * 128, 128, m128(l_src * 128)),
+            (0, 0, ymod(yw + 2) * 128, 128, 128),
             (0, 3, yw * 128, 128, m128(l_src * 128)),
             (1, 0, lax.div(ymod(yw + 2), 2) * 256, 256, 0),
             (1, 3, lax.div(yw, 2) * 256, 256, 0),
         ]
         hop = [
-            (0, 0, ymod(yw + 2) * 128, 128, m128(l_src * 128)),
+            (0, 0, ymod(yw + 2) * 128, 128, 0),
             (0, 2, ymod(yw + 1) * 128, 128, 0),
             (0, 2, ymod(yw + 3) * 128, 128, 128),
             (0, 3, yw * 128, 128, m128(l_src * 128)),
@@ -227,20 +227,26 @@
 
     def c_copies(p, j, t, arriving):
         rows = pl.ds(t * TM, TM)
-        if j == 0:
-            return [remote(send.at[p, 0, rows], recv.at[p, 1, rows], cS.at[p], cR.at[p, 0, t], y_of[1])]
         made = []
         for q in range(2):
+            k = 2 * j + q
+            if j == 0:
+                made.append(
+                    remote(
+                        send.at[p, 0, rows, pl.ds(q * 128, 128)], relay.at[p, q, rows],
+                        cS.at[p], cR.at[p, k, t], y_of[2 * q],
+                    )
+                )
+                continue
             if p == 0:
                 which = lo if (j == 1) != arriving else 1 - lo
                 place = m128(which * 128)
             else:
                 place = (j - 1) * 128
-            k = 1 + (j - 1) * 2 + q
             made.append(
                 remote(
                     send.at[p, j, rows, pl.ds(q * 128, 128)],
-                    recv.at[p, 2 * q, rows, pl.ds(place, 128)],
+                    recv.at[p, q, rows, pl.ds(place, 128)],
                     cS.at[p], cR.at[p, k, t], y_of[2 * q],
                 )
             )
@@ -252,6 +258,12 @@
         def body(t, carry):
             rows = pl.ds(t * TM if isinstance(t, int) else pl.multiple_of(t * TM, TM), TM)
             acc = jnp.dot(A[p, rows, :], B[p, j].reshape(2048, 256), preferred_element_type=jnp.float32)
+            if j in (1, 2):
+                q = j - 1
+                c_copies(p, 0, t, True)[q].wait_recv()
+                halves = [acc[:, :128], acc[:, 128:]]
+                halves[q] = halves[q] + relay[p, q, rows, :].astype(jnp.float32)
+                acc = jnp.concatenate(halves, axis=1)
             if j < 3:
                 send[p, j, rows, :] = acc.astype(BF16)
                 for copy in c_copies(p, j, t, False):
@@ -284,10 +296,10 @@
 
     def finish(p, t, rows, acc):
         if True:
-            for jj in range(3):
+            for jj in (1, 2):
                 for copy in c_copies(p, jj, t, True):
                     copy.wait_recv()
-            for d in range(3):
+            for d in range(2):
                 acc = acc + recv[p, d, rows, :].astype(jnp.float32)
             if p == 0:
                 A[1, rows, pl.ds(m128(strip(c, x)), 256)] = acc.astype(BF16)
@@ -332,23 +344,25 @@
         5: [do(x_forwards, 0, (3,))],
         7: [do(x_rest, 0, 1)],
         8: [do(x_far, 0, 1)],
-        10: [do(z_last, 1), do(d_all, 0, (0, 1)), do(compute, 1, 0, 4), do(z_last, 0), do(compute, 0, 0, 2)],
-        11: [do(compute, 0, 2, 4)],
+        9: [do(d_all, 0, (0, 1))],
+        10: [do(z_last, 0), do(compute, 0, 0, 4)],
+        11: [do(z_last, 1), do(compute, 1, 0, 2)],
+        12: [do(compute, 1, 2, 4)],
         14: [do(z_last, 2), do(compute, 2, 0, 1)],
         16: [do(compute, 2, 1, 4)],
         18: [do(z_last, 3), do(compute, 3, 0, 1), do(x_send_tile, 0), do(compute, 3, 1, 2), do(x_send_tile, 1),
-             do(compute, 3, 2, 3)],
-        19: [do(compute, 3, 3, 4), do(x_forwards, 1, (0, 1)), do(x_send_tile, 2)],
+             do(compute, 3, 2, 4)],
+        19: [do(x_forwards, 1, (0, 1)), do(x_send_tile, 2)],
         20: [do(x_forwards, 1, (2, 3)), do(x_send_tile, 3), do(x_rest, 1, 0)],
         22: [do(x_rest, 1, 1), do(x_far, 1, 0)],
         23: [do(x_forwards, 1, (4, 5)), do(z_last, 4), do(d_all, 1, (0,)), do(compute, 4, 0, 1), do(x_far, 1, 1)],
         24: [do(x_rest, 1, 2), do(x_forwards, 1, (6, 7)), do(d_all, 1, (1,)), do(compute, 4, 1, 2)],
         25: [do(x_far, 1, 2)],
         26: [do(x_rest, 1, 3)],
-        27: [do(d_all, 1, (2,)), do(compute, 4, 2, 3), do(x_far, 1, 3), do(z_last, 5), do(compute, 5, 0, 2), do(d_all, 1, (3,)),
-             do(compute, 4, 3, 4), do(compute, 5, 2, 4)],
-        29: [do(z_last, 6), do(compute, 6, 0, 1)],
-        30: [do(compute, 6, 1, 4)],
+        27: [do(d_all, 1, (2,)), do(compute, 4, 2, 3), do(x_far, 1, 3), do(z_last, 5), do(compute, 5, 0, 1), do(d_all, 1, (3,)),
+             do(compute, 4, 3, 4), do(compute, 5, 1, 2)],
+        28: [do(compute, 5, 2, 4)],
+        30: [do(z_last, 6), do(compute, 6, 0, 4)],
         31: [do(z_minor, 7), do(compute, 7, 0, 4), do(z_major, 7), do(finish_last, 0, 4)],
     }
     for i, (s, level) in enumerate(ORDER):
@@ -382,11 +396,12 @@
             pltpu.VMEM((2, 128, 256), BF16),
             pltpu.VMEM((1024, 256), jnp.float32),
             pltpu.VMEM((2, 3, 1024, 256), BF16),
-            pltpu.VMEM((2, 3, 1024, 256), BF16),
+            pltpu.VMEM((2, 2, 1024, 256), BF16),
+            pltpu.VMEM((2, 2, 1024, 128), BF16),
             dma((2,)), dma((FIRST[8],)),
             dma((2,)), dma((36,)),
             dma((2,)), dma((24,)),
-            dma((2,)), dma((2, 5, TILES)),
+            dma((2,)), dma((2, 6, TILES)),
             dma(()), dma((8,)),
             dma(()), dma((2,)),
             dma((7,)),

time: 99.4 us -> 98.3 us (0.989)
  Pallas kernels: 97.5 us -> 95.4 us
    pallas_call x1, Pallas kernels: 97.5 us -> 95.4 us  [per_device(): pl.pallas_call(kernel, out_shape=jax.ShapeDtypeStruct((rows, width), BF16...]
where the time goes in v4:
time: 98.3 us; the launch traced here: 97.2 us
  Pallas kernels  95.4 us (97%)
  local copies, waits for them, and re-layouts  1.84 us (2%)
    pallas_call x1, Pallas kernels, per_device(): pl.pallas_call(kernel, out_shape=jax.ShapeDtypeStruct((rows, width), BF16...  95.4 us

profile of v4, /device:TPU:1, one launch (start us, length us, event | category | flops | bytes accessed | tf_op | source)
XLA Modules:
  0.0 97.2 jit_solution(10600021030132490582)
XLA Ops:
  0.0 0.0 copy-start
  0.0 1.0 %copy-done = bf16[1024,256]{1,0:T(8,128)(2,1)S(1)} copy-done((bf16[1024,256]{1,0:T(8,128)(2,1)S(1)}, bf16[1024,256]{1,0:T(8,128)(2,1)}, u32[]{:S(2)}) %copy-start) | copy-done | bytes 524312
  1.0 95.4 %shard_map.37 = bf16[1024,256]{1,0:T(8,128)(2,1)S(1)} custom-call(bf16[1024,256]{1,0:T(8,128)(2,1)S(1)} %copy-done, bf16[2,512,512]{2,1,0:T(8,128)(2,1)} %bitcast.2, bf16[2,512,512]{2,1,0:T(8,128)(2,1)} %bitcast.3), custom_call_target="tpu_custom_call" | custom-call | tf_op jit(solution)/shard_map/pallas_call | solution.py:388
  96.4 0.8 copy.5
Async XLA Ops:
  0.0 1.0 %copy-start = (bf16[1024,256]{1,0:T(8,128)(2,1)S(1)}, bf16[1024,256]{1,0:T(8,128)(2,1)}, u32[]{:S(2)}) copy-start(bf16[1024,256]{1,0:T(8,128)(2,1)} %left.1) | copy-start | bytes 1572868

commit v5 on v4

--- a/solution.py
+++ b/solution.py
@@ -15,10 +15,10 @@
 
 ORDER = [
     (1, 0), (0, 0), (1, 1), (0, 1), (1, 2), (0, 2), (1, 3), (2, 0), (0, 3), (2, 1), (3, 0),
-    (2, 2), (3, 1), (2, 3), (3, 2), (3, 3), (4, 0), (4, 1), (5, 0), (4, 2), (5, 1), (4, 3),
+    (2, 2), (3, 1), (2, 3), (3, 2), (4, 0), (3, 3), (4, 1), (5, 0), (4, 2), (5, 1), (4, 3),
     (6, 0), (5, 2), (6, 1), (5, 3), (7, 0), (6, 2), (7, 1), (6, 3), (7, 2), (7, 3),
 ]
-PARTS = (1, 1, 1, 2, 2, 1, 1, 2)
+PARTS = (1, 1, 1, 1, 2, 1, 1, 2)
 FIRST = [sum(14 * n for n in PARTS[:s]) for s in range(9)]
 LAST = 7
 

time: 98.3 us -> 97.7 us (level)
  Pallas kernels: 95.4 us -> 94.3 us
    pallas_call x1, Pallas kernels: 95.4 us -> 94.3 us  [per_device(): pl.pallas_call(kernel, out_shape=jax.ShapeDtypeStruct((rows, width), BF16...]
where the time goes in v5:
time: 97.7 us; the launch traced here: 96.2 us
  Pallas kernels  94.3 us (97%)
  local copies, waits for them, and re-layouts  1.84 us (2%)
    pallas_call x1, Pallas kernels, per_device(): pl.pallas_call(kernel, out_shape=jax.ShapeDtypeStruct((rows, width), BF16...  94.3 us

profile of v5, /device:TPU:1, one launch (start us, length us, event | category | flops | bytes accessed | tf_op | source)
XLA Modules:
  0.0 96.2 jit_solution(2103321888919197425)
XLA Ops:
  0.0 0.0 copy-start
  0.0 1.0 %copy-done = bf16[1024,256]{1,0:T(8,128)(2,1)S(1)} copy-done((bf16[1024,256]{1,0:T(8,128)(2,1)S(1)}, bf16[1024,256]{1,0:T(8,128)(2,1)}, u32[]{:S(2)}) %copy-start) | copy-done | bytes 524312
  1.0 94.3 %shard_map.37 = bf16[1024,256]{1,0:T(8,128)(2,1)S(1)} custom-call(bf16[1024,256]{1,0:T(8,128)(2,1)S(1)} %copy-done, bf16[2,512,512]{2,1,0:T(8,128)(2,1)} %bitcast.2, bf16[2,512,512]{2,1,0:T(8,128)(2,1)} %bitcast.3), custom_call_target="tpu_custom_call" | custom-call | tf_op jit(solution)/shard_map/pallas_call | solution.py:388
  95.4 0.8 copy.5
Async XLA Ops:
  0.0 1.0 %copy-start = (bf16[1024,256]{1,0:T(8,128)(2,1)S(1)}, bf16[1024,256]{1,0:T(8,128)(2,1)}, u32[]{:S(2)}) copy-start(bf16[1024,256]{1,0:T(8,128)(2,1)} %left.1) | copy-start | bytes 1572868

commit v6 on v5

--- a/solution.py
+++ b/solution.py
@@ -362,8 +362,8 @@
         27: [do(d_all, 1, (2,)), do(compute, 4, 2, 3), do(x_far, 1, 3), do(z_last, 5), do(compute, 5, 0, 1), do(d_all, 1, (3,)),
              do(compute, 4, 3, 4), do(compute, 5, 1, 2)],
         28: [do(compute, 5, 2, 4)],
-        30: [do(z_last, 6), do(compute, 6, 0, 4)],
-        31: [do(z_minor, 7), do(compute, 7, 0, 4), do(z_major, 7), do(finish_last, 0, 4)],
+        30: [do(z_last, 6), do(compute, 6, 0, 2)],
+        31: [do(compute, 6, 2, 4), do(z_minor, 7), do(compute, 7, 0, 4), do(z_major, 7), do(finish_last, 0, 4)],
     }
     for i, (s, level) in enumerate(ORDER):
         z_tick(s, level)

time: 97.7 us -> 97.6 us (level)
  no operation moved by 1% of the time
where the time goes in v6:
time: 97.6 us; the launch traced here: 95.7 us
  Pallas kernels  93.8 us (96%)
  local copies, waits for them, and re-layouts  1.84 us (2%)
    pallas_call x1, Pallas kernels, per_device(): pl.pallas_call(kernel, out_shape=jax.ShapeDtypeStruct((rows, width), BF16...  93.8 us

profile of v6, /device:TPU:1, one launch (start us, length us, event | category | flops | bytes accessed | tf_op | source)
XLA Modules:
  0.0 95.7 jit_solution(4775477554794813379)
XLA Ops:
  0.0 0.0 copy-start
  0.0 1.0 %copy-done = bf16[1024,256]{1,0:T(8,128)(2,1)S(1)} copy-done((bf16[1024,256]{1,0:T(8,128)(2,1)S(1)}, bf16[1024,256]{1,0:T(8,128)(2,1)}, u32[]{:S(2)}) %copy-start) | copy-done | bytes 524312
  1.0 93.8 %shard_map.37 = bf16[1024,256]{1,0:T(8,128)(2,1)S(1)} custom-call(bf16[1024,256]{1,0:T(8,128)(2,1)S(1)} %copy-done, bf16[2,512,512]{2,1,0:T(8,128)(2,1)} %bitcast.2, bf16[2,512,512]{2,1,0:T(8,128)(2,1)} %bitcast.3), custom_call_target="tpu_custom_call" | custom-call | tf_op jit(solution)/shard_map/pallas_call | solution.py:388
  94.9 0.8 copy.5
Async XLA Ops:
  0.0 1.0 %copy-start = (bf16[1024,256]{1,0:T(8,128)(2,1)S(1)}, bf16[1024,256]{1,0:T(8,128)(2,1)}, u32[]{:S(2)}) copy-start(bf16[1024,256]{1,0:T(8,128)(2,1)} %left.1) | copy-start | bytes 1572868
